TPU v7x, 32 devices: a whole 2x2x4 slice. The times are simulated.
32 devices in a mesh: group: 2 (over y), ctx: 4 (over z), section: 2 (over x), rep: 2 (over core).
Axes of the slice: x: 2, y: 2, z: 4, core: 2. Of those that a mesh axis runs over, the one named last changes fastest.
Arguments:
- stream: bfloat16 [1024, 4096], P(('group', 'ctx'), ('section', 'rep')), parts along dimension 0, may hold values from -12 to 12
- query_proj: bfloat16 [1024, 4096], P(('group', 'ctx'), ('section', 'rep')), parts along dimension 0, may hold values from -105 to 105
- key_proj: bfloat16 [1024, 256], P(('group', 'ctx')), parts along dimension 0, may hold values from -4 to 4
- value_projected: bfloat16 [1024, 256], P(('group', 'ctx')), parts along dimension 0, may hold values from -6 to 6
- expert_ids: int32 [1024, 2], P(('group', 'ctx')), parts along dimension 0, may hold values from 0 to 3, all different within a row; in each aligned block of 128 rows (0 to 127, 128 to 255, ...) at most 80 rows name the same one
- expert_home: int32 [4], replicated, may hold values from 0 to 3, each once
- router: bfloat16 [4096, 4], P(('section', 'rep')), may hold values from -0.09375 to 0.09375
- norm_gain: bfloat16 [4096], P(('section', 'rep')), may hold values from 0.25 to 1.75
- w_gate: bfloat16 [4, 4096, 768], P('ctx', ('section', 'rep')), may hold values from -0.09375 to 0.09375
- w_up: bfloat16 [4, 4096, 768], P('ctx', ('section', 'rep')), may hold values from -0.09375 to 0.09375
- w_down: bfloat16 [4, 768, 4096], P('ctx', None, ('section', 'rep')), may hold values from -0.21875 to 0.21875
Outputs:
- result: bfloat16 [1024, 4096], P(('group', 'ctx'), ('section', 'rep')), parts along dimension 0
There are 2 independent parts, one for each index of `group`. A program takes and returns all parts, laid end to end along the dimension named above; an argument that names none is the same for every part. Nothing has to cross between parts.
Inputs may be any that keep to these rules, and one draw needn't show every extreme that they name: `expert_ids`: in each token's row the 2 experts differ; within the 128 tokens of one index of ctx no expert is chosen more than 80 times. `expert_home`: each index of ctx holds exactly one expert.
All inputs are finite; a program needn't handle non-finite values.
Results may differ from a plain program's by a relative error of at most 0.0085.
Values may be sent and summed in bfloat16 or wider, within the bound.
A program may use at most 64 MiB of HBM per device.

v0:
```python
import math

import jax
import jax.numpy as jnp
from jax import lax
from jax.sharding import PartitionSpec as P

D = 4096
HEAD_SIZE = 128
QUERY_HEADS = 32
KEY_VALUE_HEADS = 2


epsilon = 1e-06
very_negative = -1e30


def score_update(running, query_matrix, query_pos, key_block, value_block, key_anchor):
    run_max, run_sum, run_acc = running
    key_len = key_block.shape[0]
    scores = jnp.einsum(
        "tha,pa->htp", query_matrix, key_block, preferred_element_type=jnp.float32
    ) * (1.0 / math.sqrt(HEAD_SIZE))
    key_pos = key_anchor + jnp.arange(key_len, dtype=jnp.int32)
    visible = query_pos[:, None] >= key_pos[None, :]
    scores = jnp.where(visible, scores, very_negative)
    new_max = jnp.maximum(run_max, jnp.max(scores, axis=-1))
    expo = jnp.where(visible, jnp.exp(scores - new_max[..., None]), 0.0)
    factor = jnp.exp(run_max - new_max)
    new_sum = run_sum * factor + jnp.sum(expo, axis=-1)
    weights = expo.astype(jnp.bfloat16)
    new_acc = run_acc * factor[..., None] + jnp.einsum(
        "htp,pa->hta", weights, value_block, preferred_element_type=jnp.float32
    )
    return (new_max, new_sum, new_acc)


def absorb_rows(running, query_matrix, query_pos, key_rows, value_rows, anchor):
    piece_len = key_rows.shape[0]
    if piece_len > 512 and piece_len % 512 == 0:
        blocks = piece_len // 512
        key_tiles = key_rows.reshape(blocks, 512, key_rows.shape[1])
        value_tiles = value_rows.reshape(blocks, 512, value_rows.shape[1])
        anchors = anchor + 512 * jnp.arange(blocks, dtype=jnp.int32)

        def advance(state_now, tile):
            return (
                score_update(state_now, query_matrix, query_pos, tile[0], tile[1], tile[2]),
                None,
            )

        running, ignored = lax.scan(advance, running, (key_tiles, value_tiles, anchors))
        return running
    return score_update(running, query_matrix, query_pos, key_rows, value_rows, anchor)


def local(
    stream,
    query_proj,
    key_proj,
    value_projected,
    expert_ids,
    expert_home,
    router,
    norm_gain,
    w_gate,
    w_up,
    w_down,
):
    tok_rows = stream.shape[0]
    local_width = stream.shape[1]
    top_count = expert_ids.shape[1]
    columns = lax.axis_size("ctx")
    capacity = min(tok_rows, max(2, 5 * tok_rows * top_count // (4 * columns)))
    place = lax.axis_index("ctx")
    feature_index = lax.axis_index(("section", "rep"))
    heads_dev = local_width // HEAD_SIZE
    group_width = QUERY_HEADS // KEY_VALUE_HEADS
    kv_head = feature_index * heads_dev // group_width
    query_matrix = query_proj.reshape(tok_rows, heads_dev, HEAD_SIZE)
    query_pos = place * tok_rows + jnp.arange(tok_rows, dtype=jnp.int32)
    initial = (
        jnp.full((heads_dev, tok_rows), very_negative, jnp.float32),
        jnp.zeros((heads_dev, tok_rows), jnp.float32),
        jnp.zeros((heads_dev, tok_rows, HEAD_SIZE), jnp.float32),
    )
    key_single = lax.dynamic_slice_in_dim(key_proj, kv_head * HEAD_SIZE, HEAD_SIZE, 1)
    value_single = lax.dynamic_slice_in_dim(value_projected, kv_head * HEAD_SIZE, HEAD_SIZE, 1)
    run_max, run_sum, run_acc = absorb_rows(
        initial,
        query_matrix,
        query_pos,
        lax.all_gather(key_single, "ctx", axis=0, tiled=True),
        lax.all_gather(value_single, "ctx", axis=0, tiled=True),
        jnp.int32(0),
    )
    attended = jnp.transpose(run_acc / run_sum[..., None], (1, 0, 2)).reshape(tok_rows, local_width)
    hidden = stream.astype(jnp.float32) + attended
    local_sq = jnp.sum(hidden * hidden, axis=-1)
    total_sq = lax.psum(local_sq, ("section", "rep"))
    scale_rows = lax.rsqrt(total_sq / D + epsilon)
    normed = (hidden * scale_rows[:, None] * norm_gain.astype(jnp.float32)[None, :]).astype(
        jnp.bfloat16
    )
    logits = lax.psum(
        jnp.dot(normed, router, preferred_element_type=jnp.float32), ("section", "rep")
    )
    experts_all = logits.shape[1]
    one_hot = expert_ids[:, :, None] == jnp.arange(experts_all, dtype=jnp.int32)[None, None, :]
    picked = jnp.sum(jnp.where(one_hot, logits[:, None, :], 0.0), axis=-1)
    squashed = jax.nn.sigmoid(picked)
    gates = squashed / jnp.sum(squashed, axis=-1, keepdims=True)
    target = jnp.sum(jnp.where(one_hot, expert_home[None, None, :], 0), axis=-1).reshape(-1)
    target_hot = (target[:, None] == jnp.arange(columns, dtype=jnp.int32)[None, :]).astype(
        jnp.int32
    )
    running_count = jnp.cumsum(target_hot, axis=0)
    rank = jnp.sum(target_hot * (running_count - 1), axis=-1)
    slot_index = target * capacity + rank
    placing = slot_index[None, :] == jnp.arange(columns * capacity, dtype=jnp.int32)[:, None]
    placing = jnp.any(placing.reshape(columns * capacity, tok_rows, top_count), axis=-1).astype(
        jnp.bfloat16
    )
    outgoing = jnp.dot(placing, normed, preferred_element_type=jnp.float32).astype(jnp.bfloat16)
    outgoing = outgoing.reshape(columns, capacity, local_width)
    received = lax.all_to_all(outgoing, "ctx", split_axis=0, concat_axis=0, tiled=True)
    flat_rows = received.reshape(-1, local_width)
    gate_part = jnp.dot(flat_rows, w_gate[0], preferred_element_type=jnp.float32)
    up_part = jnp.dot(flat_rows, w_up[0], preferred_element_type=jnp.float32)
    gate_full = lax.psum(gate_part.astype(jnp.bfloat16), ("section", "rep")).astype(jnp.float32)
    up_full = lax.psum(up_part.astype(jnp.bfloat16), ("section", "rep")).astype(jnp.float32)
    inner = (jax.nn.silu(gate_full) * up_full).astype(jnp.bfloat16)
    answer = jnp.dot(inner, w_down[0], preferred_element_type=jnp.float32).astype(jnp.bfloat16)
    returned = lax.all_to_all(
        answer.reshape(received.shape), "ctx", split_axis=0, concat_axis=0, tiled=True
    )
    flat_back = returned.reshape(columns * capacity, local_width)
    picked_rows = flat_back[slot_index].reshape(tok_rows, top_count, local_width)
    mixed = jnp.sum(gates[:, :, None] * picked_rows.astype(jnp.float32), axis=1)
    return (hidden + mixed).astype(jnp.bfloat16)


def solution(mesh):
    placed = (
        P(("group", "ctx"), ("section", "rep")),
        P(("group", "ctx"), ("section", "rep")),
        P(("group", "ctx"), None),
        P(("group", "ctx"), None),
        P(("group", "ctx"), None),
        P(),
        P(("section", "rep"), None),
        P(("section", "rep")),
        P("ctx", ("section", "rep"), None),
        P("ctx", ("section", "rep"), None),
        P("ctx", None, ("section", "rep")),
    )
    return jax.shard_map(
        local,
        mesh=mesh,
        in_specs=placed,
        out_specs=P(("group", "ctx"), ("section", "rep")),
        check_vma=False,
    )
```

profile of v0, /device:TPU:0, one launch (start us, length us, event | category | flops | bytes accessed | tf_op | source)
XLA Modules:
  0.0 146.4 jit_solution(16333293465355152459)
XLA Ops:
  6.5 0.9 select_reduce_fusion
  7.9 0.8 constant_dynamic-slice_fusion.1
  8.6 15.1 %all_gather.6 = bf16[512,128]{1,0:T(8,128)(2,1)S(1)} all-gather(bf16[128,128]{1,0:T(8,128)(2,1)S(1)} %constant_dynamic-slice_fusion.1), channel_id=1, replica_groups=mesh['group'=2,'ctx'=4,'section'=2,'rep'=2] {'ctx'}, dimensions={0}, use_global_device_ids=true | all-gather | bytes 163840 | tf_op jit(solution)/shard_map/all_gather | solution.py:93
  23.8 1.4 fusion
  25.2 1.3 copy-done.1
  26.6 0.5 fusion.7
  27.2 12.3 %all_gather.7 = bf16[512,128]{0,1:T(8,128)(2,1)S(1)} all-gather(bf16[128,128]{0,1:T(8,128)(2,1)S(1)} %copy.40), channel_id=1, replica_groups=mesh['group'=2,'ctx'=4,'section'=2,'rep'=2] {'ctx'}, dimensions={0}, use_global_device_ids=true | all-gather | bytes 163840 | tf_op jit(solution)/shard_map/all_gather | solution.py:94
  39.5 2.3 %fusion.19 = f32[128,8,128]{0,2,1:T(8,128)S(1)} fusion(f32[512,128,8]{1,0,2:T(8,128)} %copy-done.1, f32[8,128]{1,0:T(8,128)S(1)} %get-tuple-element.8, pred[128,512]{0,1:T(8,128)(4,1)S(1)} %iota_compare_fusion.1, f32[128,8]{0,1:T(8,128)S(1)} %bitcast_add_fusion, f32[128,8]{0,1:T(8,128)S(1)} %get-tuple-element.7, bf16[512,128]{0,1:T(8,128)(2,1)S(1)} %all_gather.7), kind=kOutput, calls=%fused_computation.18 | convolution fusion | flops 137101312 | bytes 2830336 | tf_op jit(solution)/shard_map/htp,pa->hta/dot_general | solution.py:32
  41.8 0.2 copy.31
  42.2 5.7 %psum.28 = f32[128]{0:T(128)S(1)} all-reduce(f32[128]{0:T(128)S(1)} %multiply_reduce_fusion.1), channel_id=1, replica_groups=mesh['group'=2,'ctx'=4,'section'=2,'rep'=2] {'section','rep'}, use_global_device_ids=true, to_apply=%region_3.4 | all-reduce | flops 128 | bytes 1024 | tf_op jit(solution)/shard_map/psum | solution.py:100
  47.9 1.2 reduce-window.6
  49.9 0.3 convolution_convert_fusion
  50.2 21.1 %all_to_all.10 = bf16[4,80,1024]{2,1,0:T(8,128)(2,1)S(1)} all-to-all(bf16[4,80,1024]{2,1,0:T(8,128)(2,1)S(1)} %bitcast.84), channel_id=1, replica_groups=mesh['group'=2,'ctx'=4,'section'=2,'rep'=2] {'ctx'}, dimensions={0} | all-to-all | bytes 1310720 | tf_op jit(solution)/shard_map/all_to_all | solution.py:126
  71.4 1.5 fusion.12
  72.8 1.5 fusion.15
  74.3 35.2 %all-reduce.3.cloned.1.call-done = (bf16[320,768]{1,0:T(8,128)(2,1)}, bf16[320,768]{1,0:T(8,128)(2,1)}) async-done(((bf16[320,768]{1,0:T(8,128)(2,1)}, bf16[320,768]{1,0:T(8,128)(2,1)}), (bf16[320,768]{1,0:T(8,128)(2,1)}, bf16[320,768]{1,0:T(8,128)(2,1)})) %all-reduce.3.cloned.1.call-update) | async-done | bytes 983056 | tf_op jit(solution)/shard_map/psum | solution.py:131
  109.5 2.8 %fusion.9 = bf16[320,1024]{1,0:T(8,128)(2,1)} fusion(bf16[1,768,1024]{2,1,0:T(8,128)(2,1)S(1)} %copy-done, bf16[320,768]{1,0:T(8,128)(2,1)} %get-tuple-element.5, bf16[320,768]{1,0:T(8,128)(2,1)} %get-tuple-element.6), kind=kOutput, calls=%fused_computation.13 | convolution fusion | flops 505610240 | bytes 3211264 | tf_op jit(solution)/shard_map/dot_general | solution.py:133
  112.4 4.6 %all-to-all-start.1 = ((bf16[4,80,1024]{2,1,0:T(8,128)(2,1)}), bf16[4,80,1024]{2,1,0:T(8,128)(2,1)S(1)}, u32[]{:S(2)}, u32[]{:S(2)}) async-start(bf16[4,80,1024]{2,1,0:T(8,128)(2,1)} %bitcast.85), calls=%async_computation.1 | async-start | bytes 1310720 | tf_op jit(solution)/shard_map/all_to_all | solution.py:134
  117.1 5.9 %psum.29 = f32[128,4]{0,1:T(4,128)S(1)} all-reduce(f32[128,4]{0,1:T(4,128)S(1)} %fusion.45), channel_id=1, replica_groups=mesh['group'=2,'ctx'=4,'section'=2,'rep'=2] {'section','rep'}, use_global_device_ids=true, to_apply=%region_4.5 | all-reduce | flops 512 | bytes 4096 | tf_op jit(solution)/shard_map/psum | solution.py:105
  123.6 10.1 %all-to-all-done.1 = bf16[4,80,1024]{2,1,0:T(8,128)(2,1)S(1)} async-done(((bf16[4,80,1024]{2,1,0:T(8,128)(2,1)}), bf16[4,80,1024]{2,1,0:T(8,128)(2,1)S(1)}, u32[]{:S(2)}, u32[]{:S(2)}) %all-to-all-start.1) | async-done | bytes 655392 | tf_op jit(solution)/shard_map/all_to_all | solution.py:134
  133.7 2.0 %gather_fusion = bf16[256,1024]{1,0:T(8,128)(2,1)} fusion(bf16[320,1024]{1,0:T(8,128)(2,1)S(1)} %bitcast.83, s32[1024]{0:T(1024)S(1)} %pad_clamp_fusion), kind=kCustom, calls=%fused_computation | custom fusion | bytes 1049600 | tf_op jit(solution)/shard_map/gather | solution.py:138
  135.7 1.7 %reshape.137 = f32[128,2,1024]{2,1,0:T(2,128)S(1)} reshape(bf16[256,1024]{1,0:T(8,128)(2,1)} %gather_fusion) | data formatting | bytes 1572864 | tf_op jit(solution)/shard_map/convert_element_type | solution.py:139
  137.3 1.3 multiply_reduce_fusion
  138.7 0.8 add_convert_fusion
  (53 shorter events, 2.2 us)
Async XLA Ops:
  6.5 103.0 %copy-start = (bf16[1,768,1024]{2,1,0:T(8,128)(2,1)S(1)}, bf16[1,768,1024]{2,1,0:T(8,128)(2,1)}, u32[]{:S(2)}) copy-start(bf16[1,768,1024]{2,1,0:T(8,128)(2,1)} %param.21) | copy-start | bytes 4718596
  6.5 103.0 %all-reduce.3.cloned.1.call-start = ((), (), s32[]{:S(2)}) async-start(), calls=%async_computation.2 | async-start | bytes 1966080 | tf_op jit(solution)/shard_map/psum | solution.py:131
  23.8 3.3 %copy-start.3 = (bf16[128,256]{1,0:T(8,128)(2,1)S(1)}, bf16[128,256]{1,0:T(8,128)(2,1)}, u32[]{:S(2)}) copy-start(bf16[128,256]{1,0:T(8,128)(2,1)} %param.14) | copy-start | bytes 196612
  25.2 1.4 copy-start.1
  39.5 2.5 %copy-start.2 = (bf16[128,1024]{1,0:T(8,128)(2,1)S(1)}, bf16[128,1024]{1,0:T(8,128)(2,1)}, u32[]{:S(2)}) copy-start(bf16[128,1024]{1,0:T(8,128)(2,1)} %param.11) | copy-start | bytes 786436
  39.5 8.3 %copy-start.6 = (bf16[1024]{0:T(1024)(128)(2,1)S(1)}, bf16[1024]{0:T(1024)(128)(2,1)}, u32[]{:S(2)}) copy-start(bf16[1024]{0:T(1024)(128)(2,1)} %param.18) | copy-start | bytes 6148
  49.7 21.7 %copy-start.7 = (bf16[1,1024,768]{2,1,0:T(8,128)(2,1)S(1)}, bf16[1,1024,768]{2,1,0:T(8,128)(2,1)}, u32[]{:S(2)}) copy-start(bf16[1,1024,768]{2,1,0:T(8,128)(2,1)} %param.19) | copy-start | bytes 4718596
  71.4 1.5 copy-start.8
  109.5 7.4 %copy-start.4 = (bf16[1024,4]{0,1:T(4,128)(2,1)S(1)}, bf16[1024,4]{0,1:T(4,128)(2,1)}, u32[]{:S(2)}) copy-start(bf16[1024,4]{0,1:T(4,128)(2,1)} %param.17) | copy-start | bytes 24580
  109.5 13.5 %copy-start.5 = (s32[128,2]{0,1:T(2,128)S(1)}, s32[128,2]{0,1:T(2,128)}, u32[]{:S(2)}) copy-start(s32[128,2]{0,1:T(2,128)} %param.15) | copy-start | bytes 3076
  112.4 21.3 %all-to-all-start.1 = ((bf16[4,80,1024]{2,1,0:T(8,128)(2,1)}), bf16[4,80,1024]{2,1,0:T(8,128)(2,1)S(1)}, u32[]{:S(2)}, u32[]{:S(2)}) async-start(bf16[4,80,1024]{2,1,0:T(8,128)(2,1)} %bitcast.85), calls=%async_computation.1 | async-start | bytes 1310720 | tf_op jit(solution)/shard_map/all_to_all | solution.py:134
Sparse Core Ops, SparseCore 0:
  74.4 35.0 all-reduce.2
where the time goes:
time: 147 us; the launch traced here: 146 us
  blocking collectives  60.1 us (41%)
  waiting for transfers between devices  45.4 us (31%)
  between operations  13.6 us (9%)
  matrix products  9.94 us (7%)
  local copies, waits for them, and re-layouts  7.34 us (5%)
  other arithmetic  5.41 us (4%)
  starting transfers between devices  4.61 us (3%)
    psum x1, waiting for transfers between devices, local(): lax.psum(up_part.astype(jnp.bfloat16), ('section', 'rep'))  35.2 us
    all_to_all x1, blocking collectives, local(): lax.all_to_all(outgoing, 'ctx', split_axis=0, concat_axis=0, tiled=True)  21.1 us
    all_gather x1, blocking collectives, local(): lax.all_gather(key_single, 'ctx', axis=0, tiled=True)  15.1 us
    all_gather x1, blocking collectives, local(): lax.all_gather(value_single, 'ctx', axis=0, tiled=True)  12.3 us
    all_to_all x1, waiting for transfers between devices, local(): lax.all_to_all(answer.reshape(received.shape), 'ctx', split_axis=0, conca...  10.1 us
    psum x1, blocking collectives, local(): lax.psum(jnp.dot(normed, router, preferred_element_type=jnp.float32), ('s...  5.95 us
    psum x1, blocking collectives, local(): total_sq = lax.psum(local_sq, ('section', 'rep'))  5.66 us
    all_to_all x1, starting transfers between devices, local(): lax.all_to_all(answer.reshape(received.shape), 'ctx', split_axis=0, conca...  4.61 us
  transfers between devices with their start and end apart: 2, of which 2 were waited for; matrix products, arithmetic and copies ran while one was open for 0% of the time, Pallas kernels for 0%

commit v1 on v0

v1 whole, which is shorter than its diff:
```python
import functools
import math

import jax
import jax.numpy as jnp
from jax import lax
from jax.experimental import pallas as pl
from jax.experimental.pallas import tpu as pltpu
from jax.sharding import PartitionSpec as P

HEAD_SIZE = 128
epsilon = 1e-06
very_negative = -1e30
MESH = pl.DeviceIdType.MESH
F32 = jnp.float32
BF16 = jnp.bfloat16


def dot(a, b):
    return jnp.dot(a, b, preferred_element_type=F32)


def body(
    C, S, R, cap,
    stream_ref, q_ref, k_ref, v_ref, ids_ref, home_ref, router_ref, gain_ref,
    wg_hbm, wu_hbm, wd_hbm,
    out_ref,
    wg, wu, wd, qs, kbuf, vbuf, sbuf, mbuf, lbuf, acc, hid, nrm, ssbuf, lgbuf,
    place, dsrc, dbuf, asrc, abuf, bsrc, bbuf, ibuf, ysrc, ybuf,
    w_sem, k_send, k_recv, v_send, v_recv, ss_send, ss_recv, lg_send, lg_recv,
    d_send, d_recv, a_send, a_recv, b_send, b_recv, i_send, i_recv, y_send, y_recv,
):
    T, W = stream_ref.shape
    H = W // HEAD_SIZE
    F = S * R
    E = router_ref.shape[1]
    HID = wg.shape[1]
    HR = HID // R
    top = ids_ref.shape[1]
    me = lax.axis_index("ctx")
    sec = lax.axis_index("section")
    rep = lax.axis_index("rep")
    f = sec * R + rep
    kv_heads = k_ref.shape[1] // HEAD_SIZE
    kv = f * H // (H * F // kv_heads)

    def ctx_dev(d):
        return {"ctx": lax.rem(me + d + C, C)}

    def feat(j):
        return lax.rem(f + j, F)

    def feat_dev(j):
        g = feat(j)
        return {"section": g // R, "rep": lax.rem(g, R)}

    def rc(src, dst, ss, rs, dev):
        return pltpu.make_async_remote_copy(
            src_ref=src, dst_ref=dst, send_sem=ss, recv_sem=rs,
            device_id=dev, device_id_type=MESH,
        )

    weights = [
        pltpu.make_async_copy(wg_hbm.at[0], wg, w_sem.at[0]),
        pltpu.make_async_copy(wu_hbm.at[0], wu, w_sem.at[1]),
        pltpu.make_async_copy(wd_hbm.at[0], wd, w_sem.at[2]),
    ]
    for c in weights:
        c.start()

    barrier = pltpu.get_barrier_semaphore()
    for d in range(1, C):
        pl.semaphore_signal(barrier, inc=1, device_id=ctx_dev(d), device_id_type=MESH)
    for j in range(1, F):
        pl.semaphore_signal(barrier, inc=1, device_id=feat_dev(j), device_id_type=MESH)
    pl.semaphore_wait(barrier, C - 1 + F - 1)

    kcols = pl.ds(pl.multiple_of(kv * HEAD_SIZE, HEAD_SIZE), HEAD_SIZE)

    def kcopy(d):
        return rc(k_ref.at[:, kcols], kbuf.at[d], k_send.at[d], k_recv.at[d], ctx_dev(d))

    def vcopy(d):
        return rc(v_ref.at[:, kcols], vbuf.at[d], v_send.at[d], v_recv.at[d], ctx_dev(d))

    @pl.loop(1, C - me)
    def _(d):
        kcopy(d).start()

    @pl.loop(1, C - me)
    def _(d):
        vcopy(d).start()

    kbuf[0] = k_ref[:, kcols]
    vbuf[0] = v_ref[:, kcols]
    for h in range(H):
        qs[h * T : (h + 1) * T, :] = q_ref[:, h * HEAD_SIZE : (h + 1) * HEAD_SIZE]
    scale = 1.0 / math.sqrt(HEAD_SIZE)

    def scores(d):
        return (
            lax.dot_general(
                qs[...], kbuf[d], (((1,), (1,)), ((), ())), preferred_element_type=F32
            )
            * scale
        )

    row_t = lax.broadcasted_iota(jnp.int32, (T, T), 0)
    col_t = lax.broadcasted_iota(jnp.int32, (T, T), 1)
    s0 = scores(0)
    seen = jnp.concatenate([row_t >= col_t] * H, axis=0)
    s0 = jnp.where(seen, s0, very_negative)
    sbuf[0] = s0
    mbuf[...] = s0

    ids = ids_ref[...]
    dest = jnp.zeros_like(ids)
    for e in range(E):
        dest = jnp.where(ids == e, home_ref[e], dest)
    rel = dest - me
    rel = jnp.where(rel < 0, rel + C, rel)
    lanes = lax.broadcasted_iota(jnp.int32, (T, 128), 1)
    hot = jnp.zeros((T, 128), F32)
    for k in range(top):
        hot = hot + jnp.where(rel[:, k : k + 1] == lanes, 1.0, 0.0)
    lower = jnp.where(row_t > col_t, 1.0, 0.0).astype(BF16)
    rank = dot(lower, hot.astype(BF16))
    slots = lax.broadcasted_iota(jnp.int32, (T, cap), 1).astype(F32)
    for d in range(C):
        chosen = (hot[:, d : d + 1] > 0.5) & (rank[:, d : d + 1] == slots)
        place[d] = jnp.where(chosen, 1.0, 0.0).astype(BF16)

    @pl.loop(1, me + 1)
    def _(d):
        kcopy(d).wait_recv()
        s = scores(d)
        sbuf[d] = s
        mbuf[...] = jnp.maximum(mbuf[...], s)

    row_max = jnp.max(mbuf[...], axis=-1, keepdims=True)
    mbuf[...] = jnp.broadcast_to(row_max, mbuf.shape)
    e0 = jnp.exp(sbuf[0] - mbuf[...])
    lbuf[...] = e0
    acc[...] = dot(e0.astype(BF16), vbuf[0])

    @pl.loop(1, me + 1)
    def _(d):
        vcopy(d).wait_recv()
        ex = jnp.exp(sbuf[d] - mbuf[...])
        lbuf[...] = lbuf[...] + ex
        acc[...] = acc[...] + dot(ex.astype(BF16), vbuf[d])

    sq = jnp.zeros((T, HEAD_SIZE), F32)
    for h in range(H):
        rows = slice(h * T, (h + 1) * T)
        cols = slice(h * HEAD_SIZE, (h + 1) * HEAD_SIZE)
        total = jnp.sum(lbuf[rows, :], axis=-1, keepdims=True)
        hv = stream_ref[:, cols].astype(F32) + acc[rows, :] / total
        hid[:, cols] = hv
        sq = sq + hv * hv
    eye = row_t == col_t

    def to_row(col):
        return jnp.sum(jnp.where(eye, col, 0.0), axis=0, keepdims=True)

    def to_col(row):
        return jnp.sum(jnp.where(eye, row, 0.0), axis=1, keepdims=True)

    ssbuf[f] = jnp.broadcast_to(to_row(jnp.sum(sq, axis=-1, keepdims=True)), (8, T))

    def sscopy(j, owner):
        return rc(ssbuf.at[owner], ssbuf.at[owner], ss_send.at[j], ss_recv.at[owner], feat_dev(j))

    def lgcopy(j, owner):
        return rc(lgbuf.at[owner], lgbuf.at[owner], lg_send.at[j], lg_recv.at[owner], feat_dev(j))

    for j in range(1, F):
        sscopy(j, f).start()
    for j in range(1, F):
        sscopy(j, feat(j)).wait_recv()
    ss = ssbuf[0]
    for g in range(1, F):
        ss = ss + ssbuf[g]
    scale_rows = lax.rsqrt(to_col(ss[0:1, :]) / (W * F) + epsilon)
    nrm[...] = (hid[...] * scale_rows * gain_ref[...].astype(F32)).astype(BF16)

    def dcopy(d):
        return rc(dsrc.at[d], dbuf.at[d], d_send.at[d], d_recv.at[d], ctx_dev(d))

    def gathered(d):
        return lax.dot_general(
            place[d], nrm[...], (((0,), (0,)), ((), ())), preferred_element_type=F32
        ).astype(BF16)

    @pl.loop(1, C)
    def _(d):
        dsrc[d] = gathered(d)
        dcopy(d).start()

    dbuf[0] = gathered(0)

    lg = dot(nrm[...], router_ref[...])
    for e in range(E):
        lgbuf[f, e : e + 1, :] = to_row(lg[:, e : e + 1])
    for j in range(1, F):
        lgcopy(j, f).start()

    for c in weights:
        c.wait()

    def rep_at(j):
        return lax.rem(rep + j, R)

    def sec_at(j):
        return lax.rem(sec + j, S)

    def acopy(d, j, owner):
        return rc(
            asrc.at[d, rep_at(j)], abuf.at[d, owner], a_send.at[d, j], a_recv.at[d, owner],
            {"rep": rep_at(j)},
        )

    def bcopy(d, j, owner):
        return rc(
            bsrc.at[d], bbuf.at[d, owner], b_send.at[d, j], b_recv.at[d, owner],
            {"section": sec_at(j)},
        )

    def icopy(d, j, owner):
        return rc(
            ibuf.at[d, owner], ibuf.at[d, owner], i_send.at[d, j], i_recv.at[d, owner],
            {"rep": rep_at(j)},
        )

    def ycopy(d):
        return rc(ysrc.at[d], ybuf.at[d], y_send.at[d], y_recv.at[d], ctx_dev(-d))

    def stage_g(d):
        x = dbuf[d]
        for r in range(R):
            cols = slice(r * HR, (r + 1) * HR)
            asrc[d, r, :, 0:HR] = dot(x, wg[:, cols]).astype(BF16)
            asrc[d, r, :, HR : 2 * HR] = dot(x, wu[:, cols]).astype(BF16)
        for j in range(1, R):
            acopy(d, j, rep).start()

    def stage_b(d):
        total = asrc[d, rep].astype(F32)
        for j in range(1, R):
            acopy(d, j, rep_at(j)).wait_recv()
            total = total + abuf[d, rep_at(j)].astype(F32)
        bsrc[d] = total.astype(BF16)
        for j in range(1, S):
            bcopy(d, j, sec).start()

    def stage_i(d):
        total = bsrc[d].astype(F32)
        for j in range(1, S):
            bcopy(d, j, sec_at(j)).wait_recv()
            total = total + bbuf[d, sec_at(j)].astype(F32)
        g = total[:, 0:HR]
        u = total[:, HR : 2 * HR]
        ibuf[d, rep] = (g * jax.nn.sigmoid(g) * u).astype(BF16)
        for j in range(1, R):
            icopy(d, j, rep).start()

    def stage_d(d):
        for j in range(1, R):
            icopy(d, j, rep_at(j)).wait_recv()
        y = dot(ibuf[d, 0], wd[0:HR, :])
        for r in range(1, R):
            y = y + dot(ibuf[d, r], wd[r * HR : (r + 1) * HR, :])
        return y.astype(BF16)

    stage_g(0)
    stage_b(0)

    def finish(d):
        stage_i(d)
        y = stage_d(d)
        return y

    if C > 1:
        dcopy(1).wait_recv()
        stage_g(1)
        stage_b(1)
    ybuf[0] = finish(0)

    @pl.loop(2, C)
    def _(d):
        dcopy(d).wait_recv()
        stage_g(d)
        stage_b(d)
        ysrc[d - 1] = finish(d - 1)
        ycopy(d - 1).start()

    if C > 1:
        ysrc[C - 1] = finish(C - 1)
        ycopy(C - 1).start()

    for j in range(1, F):
        lgcopy(j, feat(j)).wait_recv()
    lt = lgbuf[0]
    for g in range(1, F):
        lt = lt + lgbuf[g]
    picked = jnp.zeros(ids.shape, F32)
    for e in range(E):
        picked = jnp.where(ids == e, to_col(lt[e : e + 1, :]), picked)
    squashed = jax.nn.sigmoid(picked)
    gates = squashed / jnp.sum(squashed, axis=-1, keepdims=True)

    def weighted(d):
        gd = jnp.sum(jnp.where(rel == d, gates, 0.0), axis=-1, keepdims=True)
        return gd * dot(place[d], ybuf[d])

    hid[...] = hid[...] + weighted(0)

    @pl.loop(1, C)
    def _(d):
        ycopy(d).wait_recv()
        hid[...] = hid[...] + weighted(d)

    out_ref[...] = hid[...].astype(BF16)

    @pl.loop(1, C - me)
    def _(d):
        kcopy(d).wait_send()
        vcopy(d).wait_send()

    for j in range(1, F):
        sscopy(j, f).wait_send()
        lgcopy(j, f).wait_send()

    @pl.loop(0, C)
    def _(d):
        for j in range(1, R):
            acopy(d, j, rep).wait_send()
            icopy(d, j, rep).wait_send()
        for j in range(1, S):
            bcopy(d, j, sec).wait_send()

    @pl.loop(1, C)
    def _(d):
        dcopy(d).wait_send()
        ycopy(d).wait_send()


def local(C, S, R, stream, q, k, v, ids, home, router, gain, w_gate, w_up, w_down):
    T, W = stream.shape
    top = ids.shape[1]
    H = W // HEAD_SIZE
    F = S * R
    E = router.shape[1]
    HID = w_gate.shape[2]
    HR = HID // R
    capacity = min(T, max(2, 5 * T * top // (4 * C)))
    cap = -(-capacity // 16) * 16
    e_rows = -(-E // 8) * 8
    DMA = pltpu.SemaphoreType.DMA
    vmem = pl.BlockSpec(memory_space=pltpu.VMEM)
    smem = pl.BlockSpec(memory_space=pltpu.SMEM)
    hbm = pl.BlockSpec(memory_space=pl.ANY)
    V = pltpu.VMEM
    return pl.pallas_call(
        functools.partial(body, C, S, R, cap),
        out_shape=jax.ShapeDtypeStruct((T, W), BF16),
        in_specs=[vmem] * 5 + [smem] + [vmem] * 2 + [hbm] * 3,
        out_specs=vmem,
        scratch_shapes=[
            V((W, HID), BF16), V((W, HID), BF16), V((HID, W), BF16),
            V((H * T, HEAD_SIZE), BF16),
            V((C, T, HEAD_SIZE), BF16), V((C, T, HEAD_SIZE), BF16),
            V((C, H * T, T), F32), V((H * T, T), F32), V((H * T, T), F32),
            V((H * T, HEAD_SIZE), F32),
            V((T, W), F32), V((T, W), BF16),
            V((F, 8, T), F32), V((F, e_rows, T), F32),
            V((C, T, cap), BF16),
            V((C, cap, W), BF16), V((C, cap, W), BF16),
            V((C, R, cap, 2 * HR), BF16), V((C, R, cap, 2 * HR), BF16),
            V((C, cap, 2 * HR), BF16), V((C, S, cap, 2 * HR), BF16),
            V((C, R, cap, HR), BF16),
            V((C, cap, W), BF16), V((C, cap, W), BF16),
            DMA((3,)),
            DMA((C,)), DMA((C,)), DMA((C,)), DMA((C,)),
            DMA((F,)), DMA((F,)), DMA((F,)), DMA((F,)),
            DMA((C,)), DMA((C,)),
            DMA((C, R)), DMA((C, R)),
            DMA((C, S)), DMA((C, S)),
            DMA((C, R)), DMA((C, R)),
            DMA((C,)), DMA((C,)),
        ],
        compiler_params=pltpu.CompilerParams(
            collective_id=0, has_side_effects=True, vmem_limit_bytes=62 * 1024 * 1024
        ),
        name="block",
    )(stream, q, k, v, ids, home, router, gain.reshape(1, W), w_gate, w_up, w_down)


def solution(mesh):
    placed = (
        P(("group", "ctx"), ("section", "rep")),
        P(("group", "ctx"), ("section", "rep")),
        P(("group", "ctx"), None),
        P(("group", "ctx"), None),
        P(("group", "ctx"), None),
        P(),
        P(("section", "rep"), None),
        P(("section", "rep")),
        P("ctx", ("section", "rep"), None),
        P("ctx", ("section", "rep"), None),
        P("ctx", None, ("section", "rep")),
    )
    return jax.shard_map(
        functools.partial(
            local, mesh.shape["ctx"], mesh.shape["section"], mesh.shape["rep"]
        ),
        mesh=mesh,
        in_specs=placed,
        out_specs=P(("group", "ctx"), ("section", "rep")),
        check_vma=False,
    )
```

time: 147 us -> 59.8 us (0.41)
  blocking collectives: 60.1 us -> 0 us
  Pallas kernels: 0 us -> 53.6 us
  waiting for transfers between devices: 45.4 us -> 0 us
  between operations: 13.6 us -> 0.01 us
  matrix products: 9.94 us -> 0 us
  other arithmetic: 5.41 us -> 0 us
  starting transfers between devices: 4.61 us -> 0 us
    pallas_call x0 -> x1, Pallas kernels: none -> 53.6 us  [local(): pl.pallas_call(functools.partial(body, C, S, R, cap), out_shape=jax.Shape...]
    psum x1 -> x0, waiting for transfers between devices: 35.2 us -> none  [local(): lax.psum(up_part.astype(jnp.bfloat16), ('section', 'rep'))]
    all_gather x2 -> x0, blocking collectives: 27.3 us -> none  [the longest x1 15.1 us: local(): lax.all_gather(key_single, 'ctx', axis=0, tiled=True)]
    all_to_all x1 -> x0, blocking collectives: 21.1 us -> none  [local(): lax.all_to_all(outgoing, 'ctx', split_axis=0, concat_axis=0, tiled=True)]
    psum x2 -> x0, blocking collectives: 11.6 us -> none  [the longest x1 5.95 us: local(): lax.psum(jnp.dot(normed, router, preferred_element_type=jnp.float32), ('s...]
    all_to_all x1 -> x0, waiting for transfers between devices: 10.1 us -> none  [local(): lax.all_to_all(answer.reshape(received.shape), 'ctx', split_axis=0, conca...]
    dot_general x7 -> x0, matrix products: 9.94 us -> none  [the longest x1 2.82 us: local(): jnp.dot(inner, w_down[0], preferred_element_type=jnp.float32)]
    all_to_all x1 -> x0, starting transfers between devices: 4.61 us -> none  [local(): lax.all_to_all(answer.reshape(received.shape), 'ctx', split_axis=0, conca...]
  transfers between devices with their start and end apart: 2 -> 0, of which waited for: 2 -> 0; matrix products, arithmetic and copies ran while one was open for 0% -> 0% of each run, Pallas kernels for 0% -> 0%
where the time goes in v1:
time: 59.8 us; the launch traced here: 59.6 us
  Pallas kernels  53.6 us (90%)
  local copies, waits for them, and re-layouts  5.92 us (10%)
    pallas_call x1, Pallas kernels, local(): pl.pallas_call(functools.partial(body, C, S, R, cap), out_shape=jax.Shape...  53.6 us
    unnamed x3, local copies, waits for them, and re-layouts  4.65 us
    reshape x1, local copies, waits for them, and re-layouts, local(): gain.reshape(1, W)  1.28 us

profile of v1, /device:TPU:0, one launch (start us, length us, event | category | flops | bytes accessed | tf_op | source)
XLA Modules:
  0.0 59.6 jit_solution(15525967888089393610)
XLA Ops:
  0.0 1.3 %reshape.3.gain_ref = bf16[1,1024]{1,0:T(2,128)(2,1)} reshape(bf16[1024]{0:T(1024)(128)(2,1)} %param.18) | data formatting | bytes 4096 | tf_op jit(solution)/shard_map/reshape | solution.py:396
  1.3 1.4 %copy.12.ids_ref = s32[128,2]{1,0:T(8,128)} copy(s32[128,2]{0,1:T(2,128)} %param.15) | data formatting | bytes 2048 | tf_op args[4]
  2.7 1.6 %copy.13.router_ref = bf16[1024,4]{1,0:T(8,128)(2,1)} copy(bf16[1024,4]{0,1:T(4,128)(2,1)} %param.17) | data formatting | bytes 16384 | tf_op args[6]
  4.3 53.6 %block.1 = bf16[128,1024]{1,0:T(8,128)(2,1)} custom-call(bf16[128,1024]{1,0:T(8,128)(2,1)} %stream_ref.1, bf16[128,1024]{1,0:T(8,128)(2,1)} %q_ref.1, bf16[128,256]{1,0:T(8,128)(2,1)} %k_ref.1, bf16[128,256]{1,0:T(8,128)(2,1)} %v_ref.1, s32[128,2]{1,0:T(8,128)} %copy.12.ids_ref, s32[4]{0:T(128)} %home_ref.1, bf16[1024,4]{1,0:T(8,128)(2,1)} %copy.13.router_ref, ...), custom_call_target="tpu_custom_call" | custom-call | tf_op jit(solution)/shard_map/block/pallas_call | solution.py:364
  57.9 1.7 %copy.15 = bf16[128,1024]{1,0:T(8,128)(2,1)} copy(bf16[128,1024]{1,0:T(8,128)(2,1)} %block.1) | data formatting | bytes 524288

commit v2 on v1

--- a/solution.py
+++ b/solution.py
@@ -22,21 +22,22 @@
 
 def body(
     C, S, R, cap,
-    stream_ref, q_ref, k_ref, v_ref, ids_ref, home_ref, router_ref, gain_ref,
+    stream_hbm, q_hbm, k_hbm, v_hbm, ids_hbm, home_ref, router_hbm, gain_hbm,
     wg_hbm, wu_hbm, wd_hbm,
     out_ref,
+    stream_ref, q_ref, k_ref, v_ref, ids_ref, router_ref, gain_ref,
     wg, wu, wd, qs, kbuf, vbuf, sbuf, mbuf, lbuf, acc, hid, nrm, ssbuf, lgbuf,
-    place, dsrc, dbuf, asrc, abuf, bsrc, bbuf, ibuf, ysrc, ybuf,
-    w_sem, k_send, k_recv, v_send, v_recv, ss_send, ss_recv, lg_send, lg_recv,
+    place, scsrc, scbuf, dsrc, dbuf, asrc, abuf, bsrc, bbuf, ibuf, ysrc, ybuf,
+    w_sem, x_sem, c_send, c_recv, k_send, k_recv, v_send, v_recv, ss_send, ss_recv, lg_send, lg_recv,
     d_send, d_recv, a_send, a_recv, b_send, b_recv, i_send, i_recv, y_send, y_recv,
 ):
     T, W = stream_ref.shape
     H = W // HEAD_SIZE
     F = S * R
-    E = router_ref.shape[1]
+    E = router_ref.shape[0]
     HID = wg.shape[1]
     HR = HID // R
-    top = ids_ref.shape[1]
+    top = ids_ref.shape[0]
     me = lax.axis_index("ctx")
     sec = lax.axis_index("section")
     rep = lax.axis_index("rep")
@@ -65,6 +66,17 @@
         pltpu.make_async_copy(wu_hbm.at[0], wu, w_sem.at[1]),
         pltpu.make_async_copy(wd_hbm.at[0], wd, w_sem.at[2]),
     ]
+    staged = [
+        pltpu.make_async_copy(src, dst, x_sem.at[i])
+        for i, (src, dst) in enumerate(
+            (
+                (k_hbm, k_ref), (v_hbm, v_ref), (q_hbm, q_ref), (ids_hbm, ids_ref),
+                (stream_hbm, stream_ref), (gain_hbm, gain_ref), (router_hbm, router_ref),
+            )
+        )
+    ]
+    for c in staged:
+        c.start()
     for c in weights:
         c.start()
 
@@ -73,6 +85,8 @@
         pl.semaphore_signal(barrier, inc=1, device_id=ctx_dev(d), device_id_type=MESH)
     for j in range(1, F):
         pl.semaphore_signal(barrier, inc=1, device_id=feat_dev(j), device_id_type=MESH)
+    staged[0].wait()
+    staged[1].wait()
     pl.semaphore_wait(barrier, C - 1 + F - 1)
 
     kcols = pl.ds(pl.multiple_of(kv * HEAD_SIZE, HEAD_SIZE), HEAD_SIZE)
@@ -91,6 +105,8 @@
     def _(d):
         vcopy(d).start()
 
+    for c in staged[2:]:
+        c.wait()
     kbuf[0] = k_ref[:, kcols]
     vbuf[0] = v_ref[:, kcols]
     for h in range(H):
@@ -112,6 +128,14 @@
     s0 = jnp.where(seen, s0, very_negative)
     sbuf[0] = s0
     mbuf[...] = s0
+
+    eye = row_t == col_t
+
+    def to_row(col):
+        return jnp.sum(jnp.where(eye, col, 0.0), axis=0, keepdims=True)
+
+    def to_col(row):
+        return jnp.sum(jnp.where(eye, row, 0.0), axis=1, keepdims=True)
 
     ids = ids_ref[...]
     dest = jnp.zeros_like(ids)
@@ -121,8 +145,9 @@
     rel = jnp.where(rel < 0, rel + C, rel)
     lanes = lax.broadcasted_iota(jnp.int32, (T, 128), 1)
     hot = jnp.zeros((T, 128), F32)
+    rel_cols = [to_col(rel[k : k + 1, :].astype(F32)).astype(jnp.int32) for k in range(top)]
     for k in range(top):
-        hot = hot + jnp.where(rel[:, k : k + 1] == lanes, 1.0, 0.0)
+        hot = hot + jnp.where(rel_cols[k] == lanes, 1.0, 0.0)
     lower = jnp.where(row_t > col_t, 1.0, 0.0).astype(BF16)
     rank = dot(lower, hot.astype(BF16))
     slots = lax.broadcasted_iota(jnp.int32, (T, cap), 1).astype(F32)
@@ -158,14 +183,6 @@
         hv = stream_ref[:, cols].astype(F32) + acc[rows, :] / total
         hid[:, cols] = hv
         sq = sq + hv * hv
-    eye = row_t == col_t
-
-    def to_row(col):
-        return jnp.sum(jnp.where(eye, col, 0.0), axis=0, keepdims=True)
-
-    def to_col(row):
-        return jnp.sum(jnp.where(eye, row, 0.0), axis=1, keepdims=True)
-
     ssbuf[f] = jnp.broadcast_to(to_row(jnp.sum(sq, axis=-1, keepdims=True)), (8, T))
 
     def sscopy(j, owner):
@@ -176,13 +193,8 @@
 
     for j in range(1, F):
         sscopy(j, f).start()
-    for j in range(1, F):
-        sscopy(j, feat(j)).wait_recv()
-    ss = ssbuf[0]
-    for g in range(1, F):
-        ss = ss + ssbuf[g]
-    scale_rows = lax.rsqrt(to_col(ss[0:1, :]) / (W * F) + epsilon)
-    nrm[...] = (hid[...] * scale_rows * gain_ref[...].astype(F32)).astype(BF16)
+    gain = gain_ref[...].astype(F32).reshape(1, W)
+    nrm[...] = (hid[...] * gain).astype(BF16)
 
     def dcopy(d):
         return rc(dsrc.at[d], dbuf.at[d], d_send.at[d], d_recv.at[d], ctx_dev(d))
@@ -198,12 +210,6 @@
         dcopy(d).start()
 
     dbuf[0] = gathered(0)
-
-    lg = dot(nrm[...], router_ref[...])
-    for e in range(E):
-        lgbuf[f, e : e + 1, :] = to_row(lg[:, e : e + 1])
-    for j in range(1, F):
-        lgcopy(j, f).start()
 
     for c in weights:
         c.wait()
@@ -253,11 +259,22 @@
         for j in range(1, S):
             bcopy(d, j, sec).start()
 
+    eye_cap = lax.broadcasted_iota(jnp.int32, (cap, cap), 0) == lax.broadcasted_iota(
+        jnp.int32, (cap, cap), 1
+    )
+
+    def ccopy(d):
+        return rc(scsrc.at[d], scbuf.at[d], c_send.at[d], c_recv.at[d], ctx_dev(d))
+
+    def rows_scale(d):
+        return jnp.sum(jnp.where(eye_cap, scbuf[d, 0:1, 0:cap], 0.0), axis=1, keepdims=True)
+
     def stage_i(d):
         total = bsrc[d].astype(F32)
         for j in range(1, S):
             bcopy(d, j, sec_at(j)).wait_recv()
             total = total + bbuf[d, sec_at(j)].astype(F32)
+        total = total * rows_scale(d)
         g = total[:, 0:HR]
         u = total[:, HR : 2 * HR]
         ibuf[d, rep] = (g * jax.nn.sigmoid(g) * u).astype(BF16)
@@ -273,7 +290,32 @@
         return y.astype(BF16)
 
     stage_g(0)
+
+    for j in range(1, F):
+        sscopy(j, feat(j)).wait_recv()
+    ss = ssbuf[0]
+    for g in range(1, F):
+        ss = ss + ssbuf[g]
+    scale_rows = lax.rsqrt(to_col(ss[0:1, :]) / (W * F) + epsilon)
+
+    def slot_scale(d):
+        return jnp.sum(jnp.where(place[d].astype(F32) > 0.5, scale_rows, 0.0), axis=0, keepdims=True)
+
+    @pl.loop(1, C)
+    def _(d):
+        scsrc[d, 0:1, 0:cap] = slot_scale(d)
+        ccopy(d).start()
+
+    scbuf[0, 0:1, 0:cap] = slot_scale(0)
+
     stage_b(0)
+
+    normed = (hid[...] * scale_rows * gain).astype(BF16)
+    lgbuf[f, 0:E, :] = lax.dot_general(
+        router_ref[...], normed, (((1,), (1,)), ((), ())), preferred_element_type=F32
+    )
+    for j in range(1, F):
+        lgcopy(j, f).start()
 
     def finish(d):
         stage_i(d)
@@ -291,10 +333,12 @@
         dcopy(d).wait_recv()
         stage_g(d)
         stage_b(d)
+        ccopy(d - 1).wait_recv()
         ysrc[d - 1] = finish(d - 1)
         ycopy(d - 1).start()
 
     if C > 1:
+        ccopy(C - 1).wait_recv()
         ysrc[C - 1] = finish(C - 1)
         ycopy(C - 1).start()
 
@@ -305,12 +349,15 @@
         lt = lt + lgbuf[g]
     picked = jnp.zeros(ids.shape, F32)
     for e in range(E):
-        picked = jnp.where(ids == e, to_col(lt[e : e + 1, :]), picked)
+        picked = jnp.where(ids == e, lt[e : e + 1, :], picked)
     squashed = jax.nn.sigmoid(picked)
-    gates = squashed / jnp.sum(squashed, axis=-1, keepdims=True)
+    gates = squashed / jnp.sum(squashed, axis=0, keepdims=True)
+    gate_cols = [to_col(gates[k : k + 1, :]) for k in range(top)]
 
     def weighted(d):
-        gd = jnp.sum(jnp.where(rel == d, gates, 0.0), axis=-1, keepdims=True)
+        gd = jnp.zeros((T, 1), F32)
+        for k in range(top):
+            gd = gd + jnp.where(rel_cols[k] == d, gate_cols[k], 0.0)
         return gd * dot(place[d], ybuf[d])
 
     hid[...] = hid[...] + weighted(0)
@@ -342,6 +389,7 @@
     @pl.loop(1, C)
     def _(d):
         dcopy(d).wait_send()
+        ccopy(d).wait_send()
         ycopy(d).wait_send()
 
 
@@ -356,6 +404,7 @@
     capacity = min(T, max(2, 5 * T * top // (4 * C)))
     cap = -(-capacity // 16) * 16
     e_rows = -(-E // 8) * 8
+    lanes = -(-cap // 128) * 128
     DMA = pltpu.SemaphoreType.DMA
     vmem = pl.BlockSpec(memory_space=pltpu.VMEM)
     smem = pl.BlockSpec(memory_space=pltpu.SMEM)
@@ -364,9 +413,11 @@
     return pl.pallas_call(
         functools.partial(body, C, S, R, cap),
         out_shape=jax.ShapeDtypeStruct((T, W), BF16),
-        in_specs=[vmem] * 5 + [smem] + [vmem] * 2 + [hbm] * 3,
+        in_specs=[hbm] * 5 + [smem] + [hbm] * 5,
         out_specs=vmem,
         scratch_shapes=[
+            V((T, W), BF16), V((T, W), BF16), V(k.shape, BF16), V(k.shape, BF16),
+            V((top, T), jnp.int32), V((E, W), BF16), V((W,), BF16),
             V((W, HID), BF16), V((W, HID), BF16), V((HID, W), BF16),
             V((H * T, HEAD_SIZE), BF16),
             V((C, T, HEAD_SIZE), BF16), V((C, T, HEAD_SIZE), BF16),
@@ -374,13 +425,13 @@
             V((H * T, HEAD_SIZE), F32),
             V((T, W), F32), V((T, W), BF16),
             V((F, 8, T), F32), V((F, e_rows, T), F32),
-            V((C, T, cap), BF16),
+            V((C, T, cap), BF16), V((C, 8, lanes), F32), V((C, 8, lanes), F32),
             V((C, cap, W), BF16), V((C, cap, W), BF16),
             V((C, R, cap, 2 * HR), BF16), V((C, R, cap, 2 * HR), BF16),
             V((C, cap, 2 * HR), BF16), V((C, S, cap, 2 * HR), BF16),
             V((C, R, cap, HR), BF16),
             V((C, cap, W), BF16), V((C, cap, W), BF16),
-            DMA((3,)),
+            DMA((3,)), DMA((7,)), DMA((C,)), DMA((C,)),
             DMA((C,)), DMA((C,)), DMA((C,)), DMA((C,)),
             DMA((F,)), DMA((F,)), DMA((F,)), DMA((F,)),
             DMA((C,)), DMA((C,)),
@@ -393,7 +444,7 @@
             collective_id=0, has_side_effects=True, vmem_limit_bytes=62 * 1024 * 1024
         ),
         name="block",
-    )(stream, q, k, v, ids, home, router, gain.reshape(1, W), w_gate, w_up, w_down)
+    )(stream, q, k, v, ids.T, home, router.T, gain, w_gate, w_up, w_down)
 
 
 def solution(mesh):

time: 59.8 us -> 52.9 us (0.88)
  local copies, waits for them, and re-layouts: 5.92 us -> 1.67 us
  Pallas kernels: 53.6 us -> 51.1 us
    unnamed x3 -> x1, local copies, waits for them, and re-layouts: 4.65 us -> 1.67 us
    pallas_call x1, Pallas kernels: 53.6 us -> 51.1 us  [local(): pl.pallas_call(functools.partial(body, C, S, R, cap), out_shape=jax.Shape...]
    reshape x1 -> x0, local copies, waits for them, and re-layouts: 1.28 us -> none  [local(): gain.reshape(1, W)]
where the time goes in v2:
time: 52.9 us; the launch traced here: 52.7 us
  Pallas kernels  51.1 us (97%)
  local copies, waits for them, and re-layouts  1.67 us (3%)
    pallas_call x1, Pallas kernels, local(): pl.pallas_call(functools.partial(body, C, S, R, cap), out_shape=jax.Shape...  51.1 us
    unnamed x1, local copies, waits for them, and re-layouts  1.67 us

profile of v2, /device:TPU:0, one launch (start us, length us, event | category | flops | bytes accessed | tf_op | source)
XLA Modules:
  0.0 52.7 jit_solution(18112219166140778643)
XLA Ops:
  0.0 51.1 %block.1 = bf16[128,1024]{1,0:T(8,128)(2,1)} custom-call(bf16[128,1024]{1,0:T(8,128)(2,1)} %stream_hbm.1, bf16[128,1024]{1,0:T(8,128)(2,1)} %q_hbm.1, bf16[128,256]{1,0:T(8,128)(2,1)} %k_hbm.1, bf16[128,256]{1,0:T(8,128)(2,1)} %v_hbm.1, s32[2,128]{1,0:T(2,128)} %bitcast.3, s32[4]{0:T(128)} %home_ref.1, bf16[4,1024]{1,0:T(4,128)(2,1)} %bitcast.2, ...), custom_call_target="tpu_custom_call" | custom-call | tf_op jit(solution)/shard_map/block/pallas_call | solution.py:413
  51.1 1.7 %copy.13 = bf16[128,1024]{1,0:T(8,128)(2,1)} copy(bf16[128,1024]{1,0:T(8,128)(2,1)} %block.1) | data formatting | bytes 524288

commit v3 on v2

--- a/solution.py
+++ b/solution.py
@@ -28,7 +28,7 @@
     stream_ref, q_ref, k_ref, v_ref, ids_ref, router_ref, gain_ref,
     wg, wu, wd, qs, kbuf, vbuf, sbuf, mbuf, lbuf, acc, hid, nrm, ssbuf, lgbuf,
     place, scsrc, scbuf, dsrc, dbuf, asrc, abuf, bsrc, bbuf, ibuf, ysrc, ybuf,
-    w_sem, x_sem, c_send, c_recv, k_send, k_recv, v_send, v_recv, ss_send, ss_recv, lg_send, lg_recv,
+    w_sem, x_sem, kf_send, kf_recv, vf_send, vf_recv, c_send, c_recv, k_send, k_recv, v_send, v_recv, ss_send, ss_recv, lg_send, lg_recv,
     d_send, d_recv, a_send, a_recv, b_send, b_recv, i_send, i_recv, y_send, y_recv,
 ):
     T, W = stream_ref.shape
@@ -91,18 +91,42 @@
 
     kcols = pl.ds(pl.multiple_of(kv * HEAD_SIZE, HEAD_SIZE), HEAD_SIZE)
 
+    shared = (H * F // kv_heads) % (H * R) == 0 and T % (16 * R) == 0
+    RK = R if shared else 1
+    TR = T // RK
+
+    def share(owner):
+        if RK == 1:
+            return slice(None)
+        return pl.ds(pl.multiple_of(owner * TR, TR), TR)
+
     def kcopy(d):
-        return rc(k_ref.at[:, kcols], kbuf.at[d], k_send.at[d], k_recv.at[d], ctx_dev(d))
+        rows = share(rep)
+        return rc(
+            k_ref.at[rows, kcols], kbuf.at[d, rows], k_send.at[d], k_recv.at[d], ctx_dev(d)
+        )
 
     def vcopy(d):
-        return rc(v_ref.at[:, kcols], vbuf.at[d], v_send.at[d], v_recv.at[d], ctx_dev(d))
+        rows = share(rep)
+        return rc(
+            v_ref.at[rows, kcols], vbuf.at[d, rows], v_send.at[d], v_recv.at[d], ctx_dev(d)
+        )
+
+    def kforward(d, j, owner):
+        part = kbuf.at[d, share(owner)]
+        return rc(
+            part, part, kf_send.at[d, j], kf_recv.at[d, owner], {"rep": lax.rem(rep + j, R)}
+        )
+
+    def vforward(d, j, owner):
+        part = vbuf.at[d, share(owner)]
+        return rc(
+            part, part, vf_send.at[d, j], vf_recv.at[d, owner], {"rep": lax.rem(rep + j, R)}
+        )
 
     @pl.loop(1, C - me)
     def _(d):
         kcopy(d).start()
-
-    @pl.loop(1, C - me)
-    def _(d):
         vcopy(d).start()
 
     for c in staged[2:]:
@@ -155,12 +179,29 @@
         chosen = (hot[:, d : d + 1] > 0.5) & (rank[:, d : d + 1] == slots)
         place[d] = jnp.where(chosen, 1.0, 0.0).astype(BF16)
 
-    @pl.loop(1, me + 1)
-    def _(d):
-        kcopy(d).wait_recv()
+    def earlier_scores(d):
+        for j in range(1, RK):
+            kforward(d, j, lax.rem(rep + j, R)).wait_recv()
         s = scores(d)
         sbuf[d] = s
         mbuf[...] = jnp.maximum(mbuf[...], s)
+
+    @pl.loop(1, me + 1)
+    def _(d):
+        kcopy(d).wait_recv()
+        for j in range(1, RK):
+            kforward(d, j, rep).start()
+        vcopy(d).wait_recv()
+        for j in range(1, RK):
+            vforward(d, j, rep).start()
+
+        @pl.when(d >= 2)
+        def _():
+            earlier_scores(d - 1)
+
+    @pl.when(me >= 1)
+    def _():
+        earlier_scores(me)
 
     row_max = jnp.max(mbuf[...], axis=-1, keepdims=True)
     mbuf[...] = jnp.broadcast_to(row_max, mbuf.shape)
@@ -170,7 +211,8 @@
 
     @pl.loop(1, me + 1)
     def _(d):
-        vcopy(d).wait_recv()
+        for j in range(1, RK):
+            vforward(d, j, lax.rem(rep + j, R)).wait_recv()
         ex = jnp.exp(sbuf[d] - mbuf[...])
         lbuf[...] = lbuf[...] + ex
         acc[...] = acc[...] + dot(ex.astype(BF16), vbuf[d])
@@ -317,29 +359,28 @@
     for j in range(1, F):
         lgcopy(j, f).start()
 
-    def finish(d):
-        stage_i(d)
-        y = stage_d(d)
-        return y
-
     if C > 1:
         dcopy(1).wait_recv()
         stage_g(1)
+    stage_i(0)
+    if C > 1:
         stage_b(1)
-    ybuf[0] = finish(0)
+    ybuf[0] = stage_d(0)
 
     @pl.loop(2, C)
     def _(d):
         dcopy(d).wait_recv()
         stage_g(d)
+        ccopy(d - 1).wait_recv()
+        stage_i(d - 1)
         stage_b(d)
-        ccopy(d - 1).wait_recv()
-        ysrc[d - 1] = finish(d - 1)
+        ysrc[d - 1] = stage_d(d - 1)
         ycopy(d - 1).start()
 
     if C > 1:
         ccopy(C - 1).wait_recv()
-        ysrc[C - 1] = finish(C - 1)
+        stage_i(C - 1)
+        ysrc[C - 1] = stage_d(C - 1)
         ycopy(C - 1).start()
 
     for j in range(1, F):
@@ -373,6 +414,12 @@
     def _(d):
         kcopy(d).wait_send()
         vcopy(d).wait_send()
+
+    @pl.loop(1, me + 1)
+    def _(d):
+        for j in range(1, RK):
+            kforward(d, j, rep).wait_send()
+            vforward(d, j, rep).wait_send()
 
     for j in range(1, F):
         sscopy(j, f).wait_send()
@@ -408,40 +455,45 @@
     DMA = pltpu.SemaphoreType.DMA
     vmem = pl.BlockSpec(memory_space=pltpu.VMEM)
     smem = pl.BlockSpec(memory_space=pltpu.SMEM)
-    hbm = pl.BlockSpec(memory_space=pl.ANY)
+    hbm = pl.BlockSpec(memory_space=pltpu.HBM)
     V = pltpu.VMEM
+    scratch = [
+        V((T, W), BF16), V((T, W), BF16), V(k.shape, BF16), V(k.shape, BF16),
+        V((top, T), jnp.int32), V((E, W), BF16), V((W,), BF16),
+        V((W, HID), BF16), V((W, HID), BF16), V((HID, W), BF16),
+        V((H * T, HEAD_SIZE), BF16),
+        V((C, T, HEAD_SIZE), BF16), V((C, T, HEAD_SIZE), BF16),
+        V((C, H * T, T), F32), V((H * T, T), F32), V((H * T, T), F32),
+        V((H * T, HEAD_SIZE), F32),
+        V((T, W), F32), V((T, W), BF16),
+        V((F, 8, T), F32), V((F, e_rows, T), F32),
+        V((C, T, cap), BF16), V((C, 8, lanes), F32), V((C, 8, lanes), F32),
+        V((C, cap, W), BF16), V((C, cap, W), BF16),
+        V((C, R, cap, 2 * HR), BF16), V((C, R, cap, 2 * HR), BF16),
+        V((C, cap, 2 * HR), BF16), V((C, S, cap, 2 * HR), BF16),
+        V((C, R, cap, HR), BF16),
+        V((C, cap, W), BF16), V((C, cap, W), BF16),
+        DMA((3,)), DMA((7,)), DMA((C, R)), DMA((C, R)), DMA((C, R)), DMA((C, R)), DMA((C,)), DMA((C,)),
+        DMA((C,)), DMA((C,)), DMA((C,)), DMA((C,)),
+        DMA((F,)), DMA((F,)), DMA((F,)), DMA((F,)),
+        DMA((C,)), DMA((C,)),
+        DMA((C, R)), DMA((C, R)),
+        DMA((C, S)), DMA((C, S)),
+        DMA((C, R)), DMA((C, R)),
+        DMA((C,)), DMA((C,)),
+    ]
+    used = sum(
+        math.prod(x.shape) * jnp.dtype(x.dtype).itemsize for x in scratch if x.dtype in (F32, BF16)
+    )
+    limit = 62 << 20
     return pl.pallas_call(
         functools.partial(body, C, S, R, cap),
         out_shape=jax.ShapeDtypeStruct((T, W), BF16),
         in_specs=[hbm] * 5 + [smem] + [hbm] * 5,
         out_specs=vmem,
-        scratch_shapes=[
-            V((T, W), BF16), V((T, W), BF16), V(k.shape, BF16), V(k.shape, BF16),
-            V((top, T), jnp.int32), V((E, W), BF16), V((W,), BF16),
-            V((W, HID), BF16), V((W, HID), BF16), V((HID, W), BF16),
-            V((H * T, HEAD_SIZE), BF16),
-            V((C, T, HEAD_SIZE), BF16), V((C, T, HEAD_SIZE), BF16),
-            V((C, H * T, T), F32), V((H * T, T), F32), V((H * T, T), F32),
-            V((H * T, HEAD_SIZE), F32),
-            V((T, W), F32), V((T, W), BF16),
-            V((F, 8, T), F32), V((F, e_rows, T), F32),
-            V((C, T, cap), BF16), V((C, 8, lanes), F32), V((C, 8, lanes), F32),
-            V((C, cap, W), BF16), V((C, cap, W), BF16),
-            V((C, R, cap, 2 * HR), BF16), V((C, R, cap, 2 * HR), BF16),
-            V((C, cap, 2 * HR), BF16), V((C, S, cap, 2 * HR), BF16),
-            V((C, R, cap, HR), BF16),
-            V((C, cap, W), BF16), V((C, cap, W), BF16),
-            DMA((3,)), DMA((7,)), DMA((C,)), DMA((C,)),
-            DMA((C,)), DMA((C,)), DMA((C,)), DMA((C,)),
-            DMA((F,)), DMA((F,)), DMA((F,)), DMA((F,)),
-            DMA((C,)), DMA((C,)),
-            DMA((C, R)), DMA((C, R)),
-            DMA((C, S)), DMA((C, S)),
-            DMA((C, R)), DMA((C, R)),
-            DMA((C,)), DMA((C,)),
-        ],
+        scratch_shapes=scratch,
         compiler_params=pltpu.CompilerParams(
-            collective_id=0, has_side_effects=True, vmem_limit_bytes=62 * 1024 * 1024
+            collective_id=0, has_side_effects=True, vmem_limit_bytes=limit
         ),
         name="block",
     )(stream, q, k, v, ids.T, home, router.T, gain, w_gate, w_up, w_down)

time: 52.9 us -> 52 us (0.983)
  Pallas kernels: 51.1 us -> 50.2 us
    pallas_call x1, Pallas kernels: 51.1 us -> 50.2 us  [local(): pl.pallas_call(functools.partial(body, C, S, R, cap), out_shape=jax.Shape...]
where the time goes in v3:
time: 52 us; the launch traced here: 51.9 us
  Pallas kernels  50.2 us (97%)
  local copies, waits for them, and re-layouts  1.67 us (3%)
    pallas_call x1, Pallas kernels, local(): pl.pallas_call(functools.partial(body, C, S, R, cap), out_shape=jax.Shape...  50.2 us
    unnamed x1, local copies, waits for them, and re-layouts  1.67 us

profile of v3, /device:TPU:0, one launch (start us, length us, event | category | flops | bytes accessed | tf_op | source)
XLA Modules:
  0.0 51.9 jit_solution(10856583946976804757)
XLA Ops:
  0.0 50.2 %block.1 = bf16[128,1024]{1,0:T(8,128)(2,1)} custom-call(bf16[128,1024]{1,0:T(8,128)(2,1)} %stream_hbm.1, bf16[128,1024]{1,0:T(8,128)(2,1)} %q_hbm.1, bf16[128,256]{1,0:T(8,128)(2,1)} %k_hbm.1, bf16[128,256]{1,0:T(8,128)(2,1)} %v_hbm.1, s32[2,128]{1,0:T(2,128)} %bitcast.3, s32[4]{0:T(128)} %home_ref.1, bf16[4,1024]{1,0:T(4,128)(2,1)} %bitcast.2, ...), custom_call_target="tpu_custom_call" | custom-call | tf_op jit(solution)/shard_map/block/pallas_call | solution.py:489
  50.2 1.7 %copy.13 = bf16[128,1024]{1,0:T(8,128)(2,1)} copy(bf16[128,1024]{1,0:T(8,128)(2,1)} %block.1) | data formatting | bytes 524288

commit v4 on v3

--- a/solution.py
+++ b/solution.py
@@ -55,6 +55,15 @@
         g = feat(j)
         return {"section": g // R, "rep": lax.rem(g, R)}
 
+    def other(i):
+        return i - 1 + lax.div(i - 1 + C - me, C)
+
+    def from_slot(i):
+        return lax.rem(me - other(i) + C, C)
+
+    def back_slot(i):
+        return lax.rem(other(i) - me + C, C)
+
     def rc(src, dst, ss, rs, dev):
         return pltpu.make_async_remote_copy(
             src_ref=src, dst_ref=dst, send_sem=ss, recv_sem=rs,
@@ -360,28 +369,34 @@
         lgcopy(j, f).start()
 
     if C > 1:
-        dcopy(1).wait_recv()
-        stage_g(1)
+        first = from_slot(1)
+        dcopy(first).wait_recv()
+        stage_g(first)
     stage_i(0)
     if C > 1:
-        stage_b(1)
+        stage_b(first)
     ybuf[0] = stage_d(0)
 
+    def give_back(d):
+        ysrc[d] = stage_d(d)
+        ycopy(d).start()
+
     @pl.loop(2, C)
-    def _(d):
+    def _(i):
+        d = from_slot(i)
+        before = from_slot(i - 1)
         dcopy(d).wait_recv()
         stage_g(d)
-        ccopy(d - 1).wait_recv()
-        stage_i(d - 1)
+        ccopy(before).wait_recv()
+        stage_i(before)
         stage_b(d)
-        ysrc[d - 1] = stage_d(d - 1)
-        ycopy(d - 1).start()
+        give_back(before)
 
     if C > 1:
-        ccopy(C - 1).wait_recv()
-        stage_i(C - 1)
-        ysrc[C - 1] = stage_d(C - 1)
-        ycopy(C - 1).start()
+        last = from_slot(C - 1)
+        ccopy(last).wait_recv()
+        stage_i(last)
+        give_back(last)
 
     for j in range(1, F):
         lgcopy(j, feat(j)).wait_recv()
@@ -404,7 +419,8 @@
     hid[...] = hid[...] + weighted(0)
 
     @pl.loop(1, C)
-    def _(d):
+    def _(i):
+        d = back_slot(i)
         ycopy(d).wait_recv()
         hid[...] = hid[...] + weighted(d)
 

time: 52 us -> 52.1 us (level)
  the two profiles are of different devices: /device:TPU:0 before, /device:TPU:25 now
where the time goes in v4:
time: 52.1 us; the launch traced here: 51.9 us
  Pallas kernels  50.2 us (96%)
  local copies, waits for them, and re-layouts  1.67 us (3%)
    pallas_call x1, Pallas kernels, local(): pl.pallas_call(functools.partial(body, C, S, R, cap), out_shape=jax.Shape...  50.2 us
    unnamed x1, local copies, waits for them, and re-layouts  1.67 us

profile of v4, /device:TPU:25, one launch (start us, length us, event | category | flops | bytes accessed | tf_op | source)
XLA Modules:
  0.0 51.9 jit_solution(12919502785452697532)
XLA Ops:
  0.0 50.2 %block.1 = bf16[128,1024]{1,0:T(8,128)(2,1)} custom-call(bf16[128,1024]{1,0:T(8,128)(2,1)} %stream_hbm.1, bf16[128,1024]{1,0:T(8,128)(2,1)} %q_hbm.1, bf16[128,256]{1,0:T(8,128)(2,1)} %k_hbm.1, bf16[128,256]{1,0:T(8,128)(2,1)} %v_hbm.1, s32[2,128]{1,0:T(2,128)} %bitcast.3, s32[4]{0:T(128)} %home_ref.1, bf16[4,1024]{1,0:T(4,128)(2,1)} %bitcast.2, ...), custom_call_target="tpu_custom_call" | custom-call | tf_op jit(solution)/shard_map/block/pallas_call | solution.py:505
  50.2 1.7 %copy.13 = bf16[128,1024]{1,0:T(8,128)(2,1)} copy(bf16[128,1024]{1,0:T(8,128)(2,1)} %block.1) | data formatting | bytes 524288

commit v5 on v3

--- a/solution.py
+++ b/solution.py
@@ -408,7 +408,7 @@
         ycopy(d).wait_recv()
         hid[...] = hid[...] + weighted(d)
 
-    out_ref[...] = hid[...].astype(BF16)
+    out_ref[...] = hid[...]
 
     @pl.loop(1, C - me)
     def _(d):
@@ -488,7 +488,7 @@
     limit = 62 << 20
     return pl.pallas_call(
         functools.partial(body, C, S, R, cap),
-        out_shape=jax.ShapeDtypeStruct((T, W), BF16),
+        out_shape=jax.ShapeDtypeStruct((T, W), F32),
         in_specs=[hbm] * 5 + [smem] + [hbm] * 5,
         out_specs=vmem,
         scratch_shapes=scratch,
@@ -496,7 +496,7 @@
             collective_id=0, has_side_effects=True, vmem_limit_bytes=limit
         ),
         name="block",
-    )(stream, q, k, v, ids.T, home, router.T, gain, w_gate, w_up, w_down)
+    )(stream, q, k, v, ids.T, home, router.T, gain, w_gate, w_up, w_down).astype(BF16)
 
 
 def solution(mesh):

time: 52 us -> 52.3 us (level)
  other arithmetic: 0 us -> 1.78 us
  local copies, waits for them, and re-layouts: 1.67 us -> 0 us
    convert_element_type x0 -> x1, other arithmetic: none -> 1.78 us  [local(): return pl.pallas_call(functools.partial(body, C, S, R, cap), out_shape=ja...]
    unnamed x1 -> x0, local copies, waits for them, and re-layouts: 1.67 us -> none
where the time goes in v5:
time: 52.3 us; the launch traced here: 52.1 us
  Pallas kernels  50.3 us (96%)
  other arithmetic  1.78 us (3%)
    pallas_call x1, Pallas kernels, local(): pl.pallas_call(functools.partial(body, C, S, R, cap), out_shape=jax.Shape...  50.3 us
    convert_element_type x1, other arithmetic, local(): return pl.pallas_call(functools.partial(body, C, S, R, cap), out_shape=ja...  1.78 us

profile of v5, /device:TPU:0, one launch (start us, length us, event | category | flops | bytes accessed | tf_op | source)
XLA Modules:
  0.0 52.1 jit_solution(11351194067418010552)
XLA Ops:
  0.0 50.3 %block.1 = f32[128,1024]{1,0:T(8,128)} custom-call(bf16[128,1024]{1,0:T(8,128)(2,1)} %stream_hbm.1, bf16[128,1024]{1,0:T(8,128)(2,1)} %q_hbm.1, bf16[128,256]{1,0:T(8,128)(2,1)} %k_hbm.1, bf16[128,256]{1,0:T(8,128)(2,1)} %v_hbm.1, s32[2,128]{1,0:T(2,128)} %bitcast.3, s32[4]{0:T(128)} %home_ref.1, bf16[4,1024]{1,0:T(4,128)(2,1)} %bitcast.2, ...), custom_call_target="tpu_custom_call" | custom-call | tf_op jit(solution)/shard_map/block/pallas_call | solution.py:489
  50.3 1.8 %convert_element_type.3 = bf16[128,1024]{1,0:T(8,128)(2,1)} convert(f32[128,1024]{1,0:T(8,128)} %block.1) | non-fusion elementwise | flops 131072 | bytes 786432 | tf_op jit(solution)/shard_map/convert_element_type | solution.py:499
